TPU v7x, 32 devices: a whole 2x2x4 slice. The times are simulated.
32 devices in a mesh: dp: 8 (over z, core), tensor: 4 (over y, x).
Axes of the slice: x: 2, y: 2, z: 4, core: 2. Of those that a mesh axis runs over, the one named last changes fastest.
Arguments:
- latents: bfloat16 [88, 256, 640], P('dp', 'tensor'), may hold values from -6 to 6
- cotangent: bfloat16 [88, 256, 640], P('dp', 'tensor'), may hold values from -6 to 6
- trunc_steps: int32 [8], replicated, may hold values from 30 to 40, as said below
- timesteps: int32 [88], replicated, may hold values from 100 to 900
- tile_map: int32 [88], replicated, may hold values from 0 to 87, as said below
- gain: float32 [640], replicated, may hold values from 0.5 to 1.5
- w_value: bfloat16 [640, 2560], P(None, 'tensor'), may hold values from -0.25 to 0.25
- w_gate: bfloat16 [640, 2560], P(None, 'tensor'), may hold values from -0.25 to 0.25
- w_out: bfloat16 [640, 2560], P(None, 'tensor'), may hold values from -0.125 to 0.125
Outputs:
- placed_grad: bfloat16 [88, 256, 640], P('dp', 'tensor')
- grad_value: float32 [640, 2560], P('dp', 'tensor')
- grad_gate: float32 [640, 2560], P('dp', 'tensor')
- grad_out_proj: float32 [640, 2560], P('dp', 'tensor')
- grad_gain: float32 [640], replicated
Inputs may be any that keep to these rules, and one draw needn't show every extreme that they name: trunc_steps lies in 30 to 40, so a prompt has 1 to 11 live slots, its lowest ones. tile_map is a permutation of 0 to 87. Output slots g * 11 to g * 11 + 10 form group g; the live items go to the lowest slots of the groups, and each group receives the floor or the ceiling of (number of live items) / 8 of them.
All inputs are finite; a program needn't handle non-finite values.
Results may differ from a plain program's by a relative error of at most 0.0068.
Values may be sent and summed in bfloat16 or wider, within the bound.
A program may use at most 64 MiB of HBM per device.

v0:
```python
import jax
import jax.numpy as jnp
from jax import lax
from jax.sharding import PartitionSpec as P

eps = 1e-05


def alpha_bars():
    betas = jnp.linspace(0.00085**0.5, 0.012**0.5, 1000, dtype=jnp.float32) ** 2
    return jnp.exp(jnp.cumsum(jnp.log1p(-betas)))


def gelu_parts(inputs):
    cdf = 0.5 * (1.0 + lax.erf(inputs * 0.7071067811865476))
    density = jnp.exp(-0.5 * inputs * inputs) * 0.3989422804014327
    return (inputs * cdf, cdf + inputs * density)


def norm_backward(d_normed, grad_part, hat_part, inv_part, gain):
    d_hat = d_normed * gain
    input_grad = grad_part.astype(jnp.float32) + inv_part * (
        d_hat
        - jnp.mean(d_hat, axis=-1, keepdims=True)
        - hat_part * jnp.mean(d_hat * hat_part, axis=-1, keepdims=True)
    )
    gain_local = jnp.sum(d_normed * hat_part, axis=(0, 1))
    return (input_grad, gain_local)


def tile_backward(tiles, cot_tiles, slot_times, live_count, gain, w_value, w_gate, w_out):
    full_x, full_cot = (
        lax.all_gather(tiles, "tensor", axis=1, tiled=True),
        lax.all_gather(cot_tiles, "tensor", axis=1, tiled=True),
    )
    width = full_x.shape[2]
    local_rows = tiles.shape[1]
    inner = w_value.shape[1]
    slot_total = full_x.shape[0]
    table = alpha_bars()
    picked = jnp.sum(
        jnp.where(
            slot_times[:, None] == jnp.arange(1000, dtype=jnp.int32)[None, :], table[None, :], 0.0
        ),
        axis=1,
    )
    noise_scale = jnp.sqrt(1.0 - picked)
    x_float = full_x.astype(jnp.float32)
    row_mean = jnp.mean(x_float, axis=-1, keepdims=True)
    centred = x_float - row_mean
    row_var = jnp.mean(centred * centred, axis=-1, keepdims=True)
    inv_std = lax.rsqrt(row_var + eps)
    x_hat = centred * inv_std
    normed = (x_hat * gain).astype(jnp.bfloat16)
    grad_tile = (full_cot.astype(jnp.float32) * noise_scale[:, None, None]).astype(jnp.bfloat16)
    first_dims = (((0,), (0,)), ((), ()))
    last_dims = (((1,), (1,)), ((), ()))

    def one_slot(slot_idx, carry):
        acc_wv, acc_wg, acc_wo, normed_buf = carry
        norm_tile = lax.dynamic_index_in_dim(normed, slot_idx, 0, keepdims=False)
        grad_one = lax.dynamic_index_in_dim(grad_tile, slot_idx, 0, keepdims=False)
        values_proj = jnp.dot(norm_tile, w_value, preferred_element_type=jnp.float32)
        gate_proj = jnp.dot(norm_tile, w_gate, preferred_element_type=jnp.float32)
        gelu_gate, gelu_slope = gelu_parts(gate_proj)
        hidden = (values_proj * gelu_gate).astype(jnp.bfloat16)
        d_hidden = jnp.dot(grad_one, w_out, preferred_element_type=jnp.float32)
        d_value = (d_hidden * gelu_gate).astype(jnp.bfloat16)
        d_gate = (d_hidden * values_proj * gelu_slope).astype(jnp.bfloat16)
        acc_wv = acc_wv + lax.dot_general(
            norm_tile, d_value, first_dims, preferred_element_type=jnp.float32
        )
        acc_wg = acc_wg + lax.dot_general(
            norm_tile, d_gate, first_dims, preferred_element_type=jnp.float32
        )
        acc_wo = acc_wo + lax.dot_general(
            grad_one, hidden, first_dims, preferred_element_type=jnp.float32
        )
        d_normed = lax.dot_general(d_value, w_value, last_dims, preferred_element_type=jnp.float32)
        d_normed = d_normed + lax.dot_general(
            d_gate, w_gate, last_dims, preferred_element_type=jnp.float32
        )
        normed_buf = lax.dynamic_update_index_in_dim(normed_buf, d_normed, slot_idx, 0)
        return (acc_wv, acc_wg, acc_wo, normed_buf)

    zero_w = jnp.zeros((width, inner), jnp.float32)
    init = (zero_w, zero_w, zero_w, jnp.zeros(full_x.shape, jnp.float32))
    acc_wv, acc_wg, acc_wo, normed_buf = lax.fori_loop(0, live_count, one_slot, init)
    offset = lax.axis_index("tensor") * local_rows
    hat_part = lax.dynamic_slice_in_dim(x_hat, offset, local_rows, 1)
    inv_part = lax.dynamic_slice_in_dim(inv_std, offset, local_rows, 1)
    grad_part = lax.dynamic_slice_in_dim(grad_tile, offset, local_rows, 1)
    slot_live = (jnp.arange(slot_total, dtype=jnp.int32) < live_count)[:, None, None]
    d_normed = lax.psum_scatter(normed_buf, "tensor", scatter_dimension=1, tiled=True)
    input_grad, gain_local = norm_backward(d_normed, grad_part, hat_part, inv_part, gain)
    input_grad = jnp.where(slot_live, input_grad, 0.0).astype(jnp.bfloat16)
    return (input_grad, (acc_wv, acc_wg, acc_wo), gain_local)


def per_device(latents, cotangent, trunc_steps, timesteps, tile_map, gain, w_value, w_gate, w_out):
    slot_total = latents.shape[0]
    total = tile_map.shape[0]
    my_group = lax.axis_index("dp")
    item_ids = jnp.arange(total, dtype=jnp.int32)
    live_all = (item_ids % slot_total < jnp.repeat(trunc_steps, slot_total) - 29).astype(jnp.int32)
    my_slots = my_group * slot_total + jnp.arange(slot_total, dtype=jnp.int32)
    is_mine = tile_map[:, None] == my_slots[None, :]
    dest_source = jnp.sum(jnp.where(is_mine, item_ids[:, None], 0), axis=0)
    every_x, every_cot = (
        lax.all_gather(latents, "dp", axis=0, tiled=True),
        lax.all_gather(cotangent, "dp", axis=0, tiled=True),
    )
    tiles = jnp.take(every_x, dest_source, axis=0)
    cot_tiles = jnp.take(every_cot, dest_source, axis=0)
    slot_times = jnp.take(timesteps, dest_source)
    live_count = jnp.sum(jnp.take(live_all, dest_source))
    placed_grad, weight_parts, gain_local = tile_backward(
        tiles, cot_tiles, slot_times, live_count, gain, w_value, w_gate, w_out
    )
    grad_value, grad_gate, grad_out_proj = (
        lax.psum_scatter(weight_parts[0], "dp", scatter_dimension=0, tiled=True),
        lax.psum_scatter(weight_parts[1], "dp", scatter_dimension=0, tiled=True),
        lax.psum_scatter(weight_parts[2], "dp", scatter_dimension=0, tiled=True),
    )
    grad_gain = lax.psum(gain_local, ("dp", "tensor"))
    return (placed_grad, grad_value, grad_gate, grad_out_proj, grad_gain)


def solution(mesh):
    in_specs = (
        P("dp", "tensor", None),
        P("dp", "tensor", None),
        P(),
        P(),
        P(),
        P(),
        P(None, "tensor"),
        P(None, "tensor"),
        P(None, "tensor"),
    )
    out_specs = (
        P("dp", "tensor", None),
        P("dp", "tensor"),
        P("dp", "tensor"),
        P("dp", "tensor"),
        P(),
    )
    return jax.shard_map(
        per_device, mesh=mesh, in_specs=in_specs, out_specs=out_specs, check_vma=False
    )
```

profile of v0, /device:TPU:0, one launch (start us, length us, event | category | flops | bytes accessed | tf_op | source)
XLA Modules:
  0.0 568.1 jit_solution(17423337908804927241)
XLA Ops:
  10.3 74.4 %all-gather.9.cloned.1.call-done = bf16[88,64,640]{2,1,0:T(8,128)(2,1)} async-done(((bf16[11,64,640]{2,1,0:T(8,128)(2,1)}), bf16[88,64,640]{2,1,0:T(8,128)(2,1)}) %all-gather.9.cloned.1.call-update) | async-done | bytes 7208976 | tf_op jit(solution)/shard_map/all_gather | solution.py:110
  84.7 3.8 gather_fusion.3
  88.4 68.8 %all-gather.5.cloned.1.call-done = bf16[88,64,640]{2,1,0:T(8,128)(2,1)} async-done(((bf16[11,64,640]{2,1,0:T(8,128)(2,1)}), bf16[88,64,640]{2,1,0:T(8,128)(2,1)}) %all-gather.5.cloned.1.call-update) | async-done | bytes 7208976 | tf_op jit(solution)/shard_map/all_gather | solution.py:111
  157.2 3.8 gather_fusion.1
  165.5 43.4 %all-gather.11.cloned.1.call-done = bf16[11,256,640]{2,1,0:T(8,128)(2,1)} async-done(((bf16[11,64,640]{2,1,0:T(8,128)(2,1)}), bf16[11,256,640]{2,1,0:T(8,128)(2,1)}) %all-gather.11.cloned.1.call-update) | async-done | bytes 3604496 | tf_op jit(solution)/shard_map/all_gather | solution.py:33
  208.9 2.7 convert_reduce_fusion
  213.4 45.5 %all-gather.7.cloned.1.call-done = bf16[11,256,640]{2,1,0:T(8,128)(2,1)} async-done(((bf16[11,64,640]{2,1,0:T(8,128)(2,1)}), bf16[11,256,640]{2,1,0:T(8,128)(2,1)}) %all-gather.7.cloned.1.call-update) | async-done | bytes 3604496 | tf_op jit(solution)/shard_map/all_gather | solution.py:34
  258.9 5.0 multiply_convert_fusion.4
  263.9 4.8 fusion.32
  271.3 3.6 broadcast_in_dim.84
  274.9 101.4 %while.16 = (s32[]{:T(128)}, f32[640,640]{1,0:T(8,128)}, f32[640,640]{1,0:T(8,128)}, f32[640,640]{1,0:T(8,128)S(1)}, f32[11,256,640]{2,1,0:T(8,128)}, /*index=5*...) while((s32[]{:T(128)}, f32[640,640]{1,0:T(8,128)}, ...), condition=%wide.region_8.11_spmd, body=%wide.region_7.10_spmd.sunk | while | flops 1684684800 | bytes 56197460 | solution.py:88
  277.1 1.6 fusion.81
  278.6 1.6 multiply_convert_fusion.8
  282.3 2.0 convolution_add_fusion.8
  284.2 1.9 convolution_add_fusion.9
  289.7 1.6 fusion.81
  291.2 1.6 multiply_convert_fusion.8
  294.8 2.0 convolution_add_fusion.8
  296.8 1.9 convolution_add_fusion.9
  302.3 1.6 fusion.81
  303.9 1.6 multiply_convert_fusion.8
  307.5 2.0 convolution_add_fusion.8
  309.5 1.9 convolution_add_fusion.9
  314.9 1.6 fusion.81
  316.5 1.6 multiply_convert_fusion.8
  320.1 2.0 convolution_add_fusion.8
  322.1 1.9 convolution_add_fusion.9
  327.5 1.6 fusion.81
  329.1 1.6 multiply_convert_fusion.8
  332.7 2.0 convolution_add_fusion.8
  334.7 1.9 convolution_add_fusion.9
  340.1 1.6 fusion.81
  341.7 1.6 multiply_convert_fusion.8
  345.3 2.0 convolution_add_fusion.8
  347.3 1.9 convolution_add_fusion.9
  354.3 1.6 multiply_convert_fusion.8
  357.9 2.0 convolution_add_fusion.8
  359.9 1.9 convolution_add_fusion.9
  365.3 1.6 fusion.81
  366.9 1.6 multiply_convert_fusion.8
  370.5 2.0 convolution_add_fusion.8
  372.5 1.9 convolution_add_fusion.9
  380.2 72.1 %reduce-scatter.5.cloned.1.call-done = f32[11,64,640]{2,1,0:T(8,128)} async-done(((f32[11,256,640]{2,1,0:T(8,128)}), f32[11,64,640]{2,1,0:T(8,128)}) %reduce-scatter.5.cloned.1.call-update) | async-done | bytes 1802256 | tf_op jit(solution)/shard_map/reduce_scatter | solution.py:94
  452.4 2.8 multiply_reduce_fusion
  455.2 39.6 %psum.7 = f32[640]{0:T(1024)} all-reduce(f32[640]{0:T(1024)S(1)} %get-tuple-element.72), channel_id=1, replica_groups=mesh['dp'=8,'tensor'=4] {'dp','tensor'}, use_global_device_ids=true, to_apply=%region_16.19 | all-reduce | flops 640 | bytes 5120 | tf_op jit(solution)/shard_map/psum | solution.py:125
  494.8 3.3 select_convert_fusion
  498.1 27.6 %reduce-scatter.9.cloned.1.call-done = f32[80,640]{1,0:T(8,128)} async-done(((f32[640,640]{1,0:T(8,128)}), f32[80,640]{1,0:T(8,128)}) %reduce-scatter.9.cloned.1.call-update) | async-done | bytes 204816 | tf_op jit(solution)/shard_map/reduce_scatter | solution.py:122
  525.6 35.6 %reduce-scatter.11.cloned.1.call-done = f32[80,640]{1,0:T(8,128)} async-done(((f32[640,640]{1,0:T(8,128)}), f32[80,640]{1,0:T(8,128)}) %reduce-scatter.11.cloned.1.call-update) | async-done | bytes 204816 | tf_op jit(solution)/shard_map/reduce_scatter | solution.py:123
  (181 shorter events, 57.0 us)
Async XLA Ops:
  7.2 77.5 %all-gather.9.cloned.1.call-start = ((), (), s32[]{:S(2)}) async-start(), calls=%async_computation.6 | async-start | bytes 8110080 | tf_op jit(solution)/shard_map/all_gather | solution.py:110
  7.9 149.3 %all-gather.5.cloned.1.call-start = ((), (), s32[]{:S(2)}) async-start(), calls=%async_computation.4 | async-start | bytes 8110080 | tf_op jit(solution)/shard_map/all_gather | solution.py:111
  8.7 200.2 %all-gather.11.cloned.1.call-start = ((), (), s32[]{:S(2)}) async-start(), calls=%async_computation.7 | async-start | bytes 4505600 | tf_op jit(solution)/shard_map/all_gather | solution.py:33
  88.4 74.7 %copy-start.13 = (s32[8]{0:T(128)S(1)}, s32[8]{0:T(128)}, u32[]{:S(2)}) copy-start(s32[8]{0:T(128)} %param.17) | copy-start | bytes 100
  162.5 96.4 %all-gather.7.cloned.1.call-start = ((), (), s32[]{:S(2)}) async-start(), calls=%async_computation.5 | async-start | bytes 4505600 | tf_op jit(solution)/shard_map/all_gather | solution.py:34
  163.1 289.3 %reduce-scatter.5.cloned.1.call-start = ((), (), s32[]{:S(2)}) async-start(), calls=%async_computation.8 | async-start | bytes 9011200 | tf_op jit(solution)/shard_map/reduce_scatter | solution.py:94
  213.4 50.5 %copy-start.12 = (f32[640]{0:T(1024)S(1)}, f32[640]{0:T(1024)}, u32[]{:S(2)}) copy-start(f32[640]{0:T(1024)} %param.20) | copy-start | bytes 7684
  258.9 5.0 copy-start.9
  271.3 3.6 copy-start.1
  271.3 3.6 copy-start.2
  277.1 3.6 copy-start.6
  278.6 3.6 copy-start.4
  282.2 3.9 copy-start.7
  284.2 3.3 copy-start.5
  289.6 3.6 copy-start.6
  291.2 3.6 copy-start.4
  294.8 3.9 copy-start.7
  296.8 3.4 copy-start.5
  300.8 3.1 copy-start.10
  302.3 3.6 copy-start.6
  303.9 3.6 copy-start.4
  307.5 3.9 copy-start.7
  309.4 3.4 copy-start.5
  314.9 3.6 copy-start.6
  316.5 3.6 copy-start.4
  320.1 3.9 copy-start.7
  322.1 3.3 copy-start.5
  326.0 3.1 copy-start.10
  327.5 3.6 copy-start.6
  329.1 3.6 copy-start.4
  332.7 3.9 copy-start.7
  334.7 3.3 copy-start.5
  340.1 3.6 copy-start.6
  341.7 3.6 copy-start.4
  345.3 3.9 copy-start.7
  347.3 3.3 copy-start.5
  352.7 3.6 copy-start.6
  354.3 3.6 copy-start.4
  357.9 3.9 copy-start.7
  359.9 3.3 copy-start.5
  365.3 3.6 copy-start.6
  366.9 3.6 copy-start.4
  370.5 3.9 copy-start.7
  372.5 3.3 copy-start.5
  377.5 120.5 %reduce-scatter.7.cloned.1.call-start = ((), (), s32[]{:S(2)}) async-start(), calls=%async_computation.9 | async-start | bytes 1843200 | tf_op jit(solution)/shard_map/reduce_scatter | solution.py:121
  378.1 147.5 %reduce-scatter.9.cloned.1.call-start = ((), (), s32[]{:S(2)}) async-start(), calls=%async_computation.10 | async-start | bytes 1843200 | tf_op jit(solution)/shard_map/reduce_scatter | solution.py:122
  378.8 182.4 %reduce-scatter.11.cloned.1.call-start = ((), (), s32[]{:S(2)}) async-start(), calls=%async_computation.11 | async-start | bytes 1843200 | tf_op jit(solution)/shard_map/reduce_scatter | solution.py:123
  452.4 42.4 %copy-start.11 = (f32[11,64,640]{2,1,0:T(8,128)S(1)}, f32[11,64,640]{2,1,0:T(8,128)}, u32[]{:S(2)}) copy-start(f32[11,64,640]{2,1,0:T(8,128)} %reduce-scatter.5.cloned.1.call-done) | copy-start | bytes 5406724
  (9 other events, 25.3 us)
Sparse Core Ops, SparseCore 0:
  9.6 74.9 all-gather.8
  86.3 70.8 all-gather.4
  162.6 46.2 all-gather.10
  211.2 47.6 all-gather.6
  376.5 75.8 reduce-scatter.4
  455.1 34.5 reduce-scatter.6
  492.5 33.0 reduce-scatter.8
  528.5 32.6 reduce-scatter.10
where the time goes:
time: 570 us; the launch traced here: 568 us
  waiting for transfers between devices  371 us (65%)
  matrix products  95 us (17%)
  blocking collectives  39.6 us (7%)
  other arithmetic  24.2 us (4%)
  local copies, waits for them, and re-layouts  17.3 us (3%)
  between operations  14.3 us (3%)
  loops' own time  6.18 us (1%)
    all_gather x1, waiting for transfers between devices, per_device(): lax.all_gather(latents, 'dp', axis=0, tiled=True)  74.4 us
    reduce_scatter x1, waiting for transfers between devices, tile_backward(): lax.psum_scatter(normed_buf, 'tensor', scatter_dimension=1, tiled=True)  72.1 us
    all_gather x1, waiting for transfers between devices, per_device(): lax.all_gather(cotangent, 'dp', axis=0, tiled=True)  68.8 us
    all_gather x1, waiting for transfers between devices, tile_backward(): lax.all_gather(cot_tiles, 'tensor', axis=1, tiled=True)  45.5 us
    all_gather x1, waiting for transfers between devices, tile_backward(): lax.all_gather(tiles, 'tensor', axis=1, tiled=True)  43.4 us
    psum x1, blocking collectives, per_device(): grad_gain = lax.psum(gain_local, ('dp', 'tensor'))  39.6 us
    reduce_scatter x1, waiting for transfers between devices, per_device(): lax.psum_scatter(weight_parts[2], 'dp', scatter_dimension=0, tiled=True)  35.6 us
    reduce_scatter x1, waiting for transfers between devices, per_device(): lax.psum_scatter(weight_parts[1], 'dp', scatter_dimension=0, tiled=True)  27.6 us
  transfers between devices with their start and end apart: 8, of which 7 were waited for; matrix products, arithmetic and copies ran while one was open for 3% of the time, Pallas kernels for 0%

commit v1 on v0

--- a/solution.py
+++ b/solution.py
@@ -122,7 +122,7 @@
         lax.psum_scatter(weight_parts[1], "dp", scatter_dimension=0, tiled=True),
         lax.psum_scatter(weight_parts[2], "dp", scatter_dimension=0, tiled=True),
     )
-    grad_gain = lax.psum(gain_local, ("dp", "tensor"))
+    grad_gain = jnp.sum(lax.all_gather(gain_local, ("dp", "tensor")), axis=0)
     return (placed_grad, grad_value, grad_gate, grad_out_proj, grad_gain)
 
 

time: 570 us -> 570 us (level)
  waiting for transfers between devices: 371 us -> 343 us
  blocking collectives: 39.6 us -> 67.4 us
    all_gather x0 -> x1, blocking collectives: none -> 67.4 us  [per_device(): grad_gain = jnp.sum(lax.all_gather(gain_local, ('dp', 'tensor')), axis=0)]
    psum x1 -> x0, blocking collectives: 39.6 us -> none  [per_device(): grad_gain = lax.psum(gain_local, ('dp', 'tensor'))]
    reduce_scatter x1, waiting for transfers between devices: 27.6 us -> 0.01 us  [per_device(): lax.psum_scatter(weight_parts[1], 'dp', scatter_dimension=0, tiled=True)]
  transfers between devices with their start and end apart: 8 -> 8, of which waited for: 7 -> 6; matrix products, arithmetic and copies ran while one was open for 3% -> 3% of each run, Pallas kernels for 0% -> 0%
where the time goes in v1:
time: 570 us; the launch traced here: 568 us
  waiting for transfers between devices  343 us (60%)
  matrix products  95 us (17%)
  blocking collectives  67.4 us (12%)
  other arithmetic  24.9 us (4%)
  local copies, waits for them, and re-layouts  17.3 us (3%)
  between operations  14.3 us (3%)
  loops' own time  6.18 us (1%)
    all_gather x1, waiting for transfers between devices, per_device(): lax.all_gather(latents, 'dp', axis=0, tiled=True)  74.4 us
    reduce_scatter x1, waiting for transfers between devices, tile_backward(): lax.psum_scatter(normed_buf, 'tensor', scatter_dimension=1, tiled=True)  72.1 us
    all_gather x1, waiting for transfers between devices, per_device(): lax.all_gather(cotangent, 'dp', axis=0, tiled=True)  68.8 us
    all_gather x1, blocking collectives, per_device(): grad_gain = jnp.sum(lax.all_gather(gain_local, ('dp', 'tensor')), axis=0)  67.4 us
    all_gather x1, waiting for transfers between devices, tile_backward(): lax.all_gather(cot_tiles, 'tensor', axis=1, tiled=True)  45.5 us
    all_gather x1, waiting for transfers between devices, tile_backward(): lax.all_gather(tiles, 'tensor', axis=1, tiled=True)  43.4 us
    reduce_scatter x1, waiting for transfers between devices, per_device(): lax.psum_scatter(weight_parts[2], 'dp', scatter_dimension=0, tiled=True)  34.5 us
    dot_general x8, matrix products, one_slot(): lax.dot_general(norm_tile, d_gate, first_dims, preferred_element_type=jnp...  15.7 us
  transfers between devices with their start and end apart: 8, of which 6 were waited for; matrix products, arithmetic and copies ran while one was open for 3% of the time, Pallas kernels for 0%

profile of v1, /device:TPU:0, one launch (start us, length us, event | category | flops | bytes accessed | tf_op | source)
XLA Modules:
  0.0 567.9 jit_solution(8179840159577173374)
XLA Ops:
  10.3 74.4 %all-gather.11.cloned.1.call-done = bf16[88,64,640]{2,1,0:T(8,128)(2,1)} async-done(((bf16[11,64,640]{2,1,0:T(8,128)(2,1)}), bf16[88,64,640]{2,1,0:T(8,128)(2,1)}) %all-gather.11.cloned.1.call-update) | async-done | bytes 7208976 | tf_op jit(solution)/shard_map/all_gather | solution.py:110
  84.7 3.8 gather_fusion.3
  88.4 68.8 %all-gather.7.cloned.1.call-done = bf16[88,64,640]{2,1,0:T(8,128)(2,1)} async-done(((bf16[11,64,640]{2,1,0:T(8,128)(2,1)}), bf16[88,64,640]{2,1,0:T(8,128)(2,1)}) %all-gather.7.cloned.1.call-update) | async-done | bytes 7208976 | tf_op jit(solution)/shard_map/all_gather | solution.py:111
  157.2 3.8 gather_fusion.1
  165.5 43.4 %all-gather.13.cloned.1.call-done = bf16[11,256,640]{2,1,0:T(8,128)(2,1)} async-done(((bf16[11,64,640]{2,1,0:T(8,128)(2,1)}), bf16[11,256,640]{2,1,0:T(8,128)(2,1)}) %all-gather.13.cloned.1.call-update) | async-done | bytes 3604496 | tf_op jit(solution)/shard_map/all_gather | solution.py:33
  208.9 2.7 convert_reduce_fusion
  213.4 45.5 %all-gather.9.cloned.1.call-done = bf16[11,256,640]{2,1,0:T(8,128)(2,1)} async-done(((bf16[11,64,640]{2,1,0:T(8,128)(2,1)}), bf16[11,256,640]{2,1,0:T(8,128)(2,1)}) %all-gather.9.cloned.1.call-update) | async-done | bytes 3604496 | tf_op jit(solution)/shard_map/all_gather | solution.py:34
  258.9 5.0 multiply_convert_fusion.4
  263.9 4.8 fusion.32
  271.3 3.6 broadcast_in_dim.84
  274.9 101.4 %while.16 = (s32[]{:T(128)}, f32[640,640]{1,0:T(8,128)}, f32[640,640]{1,0:T(8,128)}, f32[640,640]{1,0:T(8,128)S(1)}, f32[11,256,640]{2,1,0:T(8,128)}, /*index=5*...) while((s32[]{:T(128)}, f32[640,640]{1,0:T(8,128)}, ...), condition=%wide.region_8.11_spmd, body=%wide.region_7.10_spmd.sunk | while | flops 1684684800 | bytes 56197460 | solution.py:88
  277.1 1.6 fusion.81
  278.6 1.6 multiply_convert_fusion.8
  282.3 2.0 convolution_add_fusion.8
  284.2 1.9 convolution_add_fusion.9
  289.7 1.6 fusion.81
  291.2 1.6 multiply_convert_fusion.8
  294.8 2.0 convolution_add_fusion.8
  296.8 1.9 convolution_add_fusion.9
  302.3 1.6 fusion.81
  303.9 1.6 multiply_convert_fusion.8
  307.5 2.0 convolution_add_fusion.8
  309.5 1.9 convolution_add_fusion.9
  314.9 1.6 fusion.81
  316.5 1.6 multiply_convert_fusion.8
  320.1 2.0 convolution_add_fusion.8
  322.1 1.9 convolution_add_fusion.9
  327.5 1.6 fusion.81
  329.1 1.6 multiply_convert_fusion.8
  332.7 2.0 convolution_add_fusion.8
  334.7 1.9 convolution_add_fusion.9
  340.1 1.6 fusion.81
  341.7 1.6 multiply_convert_fusion.8
  345.3 2.0 convolution_add_fusion.8
  347.3 1.9 convolution_add_fusion.9
  352.7 1.6 fusion.81
  354.3 1.6 multiply_convert_fusion.8
  357.9 2.0 convolution_add_fusion.8
  359.9 1.9 convolution_add_fusion.9
  365.3 1.6 fusion.81
  366.9 1.6 multiply_convert_fusion.8
  370.5 2.0 convolution_add_fusion.8
  372.5 1.9 convolution_add_fusion.9
  380.2 72.1 %reduce-scatter.5.cloned.1.call-done = f32[11,64,640]{2,1,0:T(8,128)} async-done(((f32[11,256,640]{2,1,0:T(8,128)}), f32[11,64,640]{2,1,0:T(8,128)}) %reduce-scatter.5.cloned.1.call-update) | async-done | bytes 1802256 | tf_op jit(solution)/shard_map/reduce_scatter | solution.py:94
  452.4 2.8 multiply_reduce_fusion
  455.2 67.4 %all-gather.1 = f32[32,1,640]{2,1,0:T(1,128)S(1)} all-gather(f32[1,1,640]{2,1,0:T(1,128)S(1)} %reshape.133), channel_id=2, replica_groups=mesh['dp'=8,'tensor'=4] {'dp','tensor'}, dimensions={0}, use_global_device_ids=true | all-gather | bytes 84480 | tf_op jit(solution)/shard_map/all_gather | solution.py:125
  523.2 3.3 select_convert_fusion
  526.5 34.5 %reduce-scatter.11.cloned.1.call-done = f32[80,640]{1,0:T(8,128)} async-done(((f32[640,640]{1,0:T(8,128)}), f32[80,640]{1,0:T(8,128)}) %reduce-scatter.11.cloned.1.call-update) | async-done | bytes 204816 | tf_op jit(solution)/shard_map/reduce_scatter | solution.py:123
  (183 shorter events, 56.1 us)
Async XLA Ops:
  7.2 77.5 %all-gather.11.cloned.1.call-start = ((), (), s32[]{:S(2)}) async-start(), calls=%async_computation.6 | async-start | bytes 8110080 | tf_op jit(solution)/shard_map/all_gather | solution.py:110
  7.9 149.3 %all-gather.7.cloned.1.call-start = ((), (), s32[]{:S(2)}) async-start(), calls=%async_computation.4 | async-start | bytes 8110080 | tf_op jit(solution)/shard_map/all_gather | solution.py:111
  8.7 200.2 %all-gather.13.cloned.1.call-start = ((), (), s32[]{:S(2)}) async-start(), calls=%async_computation.7 | async-start | bytes 4505600 | tf_op jit(solution)/shard_map/all_gather | solution.py:33
  88.4 74.7 %copy-start.13 = (s32[8]{0:T(128)S(1)}, s32[8]{0:T(128)}, u32[]{:S(2)}) copy-start(s32[8]{0:T(128)} %param.17) | copy-start | bytes 100
  162.5 96.4 %all-gather.9.cloned.1.call-start = ((), (), s32[]{:S(2)}) async-start(), calls=%async_computation.5 | async-start | bytes 4505600 | tf_op jit(solution)/shard_map/all_gather | solution.py:34
  163.1 289.3 %reduce-scatter.5.cloned.1.call-start = ((), (), s32[]{:S(2)}) async-start(), calls=%async_computation.8 | async-start | bytes 9011200 | tf_op jit(solution)/shard_map/reduce_scatter | solution.py:94
  213.4 50.5 %copy-start.12 = (f32[640]{0:T(1024)S(1)}, f32[640]{0:T(1024)}, u32[]{:S(2)}) copy-start(f32[640]{0:T(1024)} %param.20) | copy-start | bytes 7684
  258.9 5.0 copy-start.9
  271.3 3.6 copy-start.1
  271.3 3.6 copy-start.2
  277.1 3.6 copy-start.6
  278.6 3.6 copy-start.4
  282.2 3.9 copy-start.7
  284.2 3.3 copy-start.5
  289.6 3.6 copy-start.6
  291.2 3.6 copy-start.4
  294.8 3.9 copy-start.7
  296.8 3.4 copy-start.5
  300.8 3.1 copy-start.10
  302.3 3.6 copy-start.6
  303.9 3.6 copy-start.4
  307.5 3.9 copy-start.7
  309.4 3.4 copy-start.5
  314.9 3.6 copy-start.6
  316.5 3.6 copy-start.4
  320.1 3.9 copy-start.7
  322.1 3.3 copy-start.5
  326.0 3.1 copy-start.10
  327.5 3.6 copy-start.6
  329.1 3.6 copy-start.4
  332.7 3.9 copy-start.7
  334.7 3.3 copy-start.5
  340.1 3.6 copy-start.6
  341.7 3.6 copy-start.4
  345.3 3.9 copy-start.7
  347.3 3.3 copy-start.5
  352.7 3.6 copy-start.6
  354.3 3.6 copy-start.4
  357.9 3.9 copy-start.7
  359.9 3.3 copy-start.5
  365.3 3.6 copy-start.6
  366.9 3.6 copy-start.4
  370.5 3.9 copy-start.7
  372.5 3.3 copy-start.5
  377.5 149.0 %reduce-scatter.7.cloned.1.call-start = ((), (), s32[]{:S(2)}) async-start(), calls=%async_computation.9 | async-start | bytes 1843200 | tf_op jit(solution)/shard_map/reduce_scatter | solution.py:121
  378.1 148.5 %reduce-scatter.9.cloned.1.call-start = ((), (), s32[]{:S(2)}) async-start(), calls=%async_computation.10 | async-start | bytes 1843200 | tf_op jit(solution)/shard_map/reduce_scatter | solution.py:122
  378.8 182.2 %reduce-scatter.11.cloned.1.call-start = ((), (), s32[]{:S(2)}) async-start(), calls=%async_computation.11 | async-start | bytes 1843200 | tf_op jit(solution)/shard_map/reduce_scatter | solution.py:123
  452.4 70.8 %copy-start.11 = (f32[11,64,640]{2,1,0:T(8,128)S(1)}, f32[11,64,640]{2,1,0:T(8,128)}, u32[]{:S(2)}) copy-start(f32[11,64,640]{2,1,0:T(8,128)} %reduce-scatter.5.cloned.1.call-done) | copy-start | bytes 5406724
  (9 other events, 25.3 us)
Sparse Core Ops, SparseCore 0:
  9.6 74.9 all-gather.10
  86.3 70.8 all-gather.6
  162.6 46.2 all-gather.12
  211.2 47.6 all-gather.8
  376.5 75.8 reduce-scatter.4
  455.1 34.5 reduce-scatter.6
  492.6 32.7 reduce-scatter.8
  528.2 32.8 reduce-scatter.10
